TPU v7x, 32 devices: a whole 2x2x4 slice. The times are simulated.
32 devices in a mesh: group: 4 (over x, core), seq: 2 (over y), expert: 4 (over z).
Axes of the slice: x: 2, y: 2, z: 4, core: 2. Of those that a mesh axis runs over, the one named last changes fastest.
Arguments:
- queries: bfloat16 [16, 32, 128], P('expert', 'group')
- keys: bfloat16 [16, 256, 8, 128], P('expert', 'seq', 'group')
- values: bfloat16 [16, 256, 8, 128], P('expert', 'seq', 'group'), may hold values from -48 to 48
- block_of_slot: int32 [16, 16], P('expert', 'seq'), may hold values from 0 to 15, each once within a row
- lengths: int32 [16], P('expert'), may hold values from 128 to 256
- out_proj: bfloat16 [4096, 4096], P('group', 'seq'), may hold values from -0.09375 to 0.09375
- residual: bfloat16 [16, 4096], P('expert', 'seq'), may hold values from -6 to 6
- norm_gain: bfloat16 [4096], replicated, may hold values from 0.25 to 1.75
- router: bfloat16 [4096, 8], replicated, may hold values from -0.09375 to 0.09375
- routes: int32 [16, 2], P('expert'), may hold values from 0 to 7, all different within a row; in each aligned block of 4 rows (0 to 3, 4 to 7, ...) at most 2 rows name the same one
- w_gate: bfloat16 [8, 4096, 14336], P('expert', None, ('group', 'seq')), may hold values from -0.09375 to 0.09375
- w_up: bfloat16 [8, 4096, 14336], P('expert', None, ('group', 'seq')), may hold values from -0.09375 to 0.09375
- w_down: bfloat16 [8, 14336, 4096], P('expert', ('group', 'seq')), may hold values from -0.046875 to 0.046875
Outputs:
- layer_out: bfloat16 [16, 4096], P('expert', 'seq')
Inputs may be any that keep to these rules, and one draw needn't show every extreme that they name: `block_of_slot`: each row lists every logical block once. `routes`: the two ids of a row differ; among the 4 rows of one device no expert is named more than 2 times, and in some such blocks one expert is named exactly 2 times.
All inputs are finite; a program needn't handle non-finite values.
Results may differ from a plain program's by a relative error of at most 0.013.
Values may be sent and summed in bfloat16 or wider, within the bound.
No kernel may reach another device: no remote copies, remote signals or barrier semaphores. Data moves between devices by JAX's collectives and lax.ppermute only.
A program may use at most 128 MiB of HBM per device.

v0:
```python
import jax
import jax.numpy as jnp
from jax import lax
from jax.sharding import PartitionSpec as P

BLOCK = 16
CAPACITY = 2


masked_score = -1e30


def combined_all(value, axis, combine):
    everything = jax.tree.map(lambda part: lax.all_gather(part, axis), value)
    initial = jax.tree.map(lambda part: part[0], everything)

    def hop(k, so_far):
        return combine(so_far, jax.tree.map(lambda part: part[k], everything))

    return lax.fori_loop(1, lax.axis_size(axis), hop, initial)


def combine_carry(earlier, later):
    high_a, total_a, sums_a = earlier
    high_b, total_b, sums_b = later
    highest = jnp.maximum(high_a, high_b)
    scale_a = jnp.exp(high_a - highest)
    scale_b = jnp.exp(high_b - highest)
    return (
        highest,
        total_a * scale_a + total_b * scale_b,
        sums_a * scale_a[..., None] + sums_b * scale_b[..., None],
    )


def shards(
    queries,
    keys,
    values,
    block_of_slot,
    lengths,
    out_proj,
    residual,
    norm_gain,
    router,
    routes,
    w_gate,
    w_up,
    w_down,
):
    batch_rows, local_heads, head_dim = queries.shape
    span_len = keys.shape[1]
    kv_local = keys.shape[2]
    per_kv = local_heads // kv_local
    grouped = queries.reshape(batch_rows, kv_local, per_kv, head_dim)
    scores = jnp.einsum(
        "rkgd,rlkd->rkgl", grouped, keys, preferred_element_type=jnp.float32
    ) * head_dim ** (-0.5)
    offsets = jnp.arange(BLOCK, dtype=jnp.int32)
    position = (block_of_slot[:, :, None] * BLOCK + offsets[None, None, :]).reshape(
        batch_rows, span_len
    )
    visible = (position < lengths[:, None])[:, None, None, :]
    masked = jnp.where(visible, scores, masked_score)
    highest = jnp.max(masked, axis=-1)
    probs = jnp.where(visible, jnp.exp(masked - highest[..., None]), 0.0)
    totals = jnp.sum(probs, axis=-1)
    weighted = jnp.einsum(
        "rkgl,rlkd->rkgd", probs.astype(jnp.bfloat16), values, preferred_element_type=jnp.float32
    )
    local_carry = (highest, totals, weighted)
    highest, totals, weighted = combined_all(local_carry, "seq", combine_carry)
    attended = (
        (weighted / totals[..., None])
        .astype(jnp.bfloat16)
        .reshape(batch_rows, local_heads * head_dim)
    )
    partial_value = jnp.dot(attended, out_proj, preferred_element_type=jnp.float32)
    attention = lax.psum(partial_value, "group")
    hidden = residual.astype(jnp.float32) + attention
    full_rows = lax.all_gather(hidden, "seq", axis=1, tiled=True)
    meansq = jnp.mean(full_rows * full_rows, axis=-1, keepdims=True)
    normed = (full_rows * lax.rsqrt(meansq + 1e-05) * norm_gain.astype(jnp.float32)).astype(
        jnp.bfloat16
    )
    logits = jnp.dot(normed, router, preferred_element_type=jnp.float32)
    experts = router.shape[1]
    onehot = (routes[:, :, None] == jnp.arange(experts, dtype=jnp.int32)[None, None, :]).astype(
        jnp.int32
    )
    chosen = jnp.sum(onehot.astype(jnp.float32) * logits[:, None, :], axis=-1)
    gate_probs = jax.nn.softmax(chosen, axis=-1)
    per_row = jnp.sum(onehot, axis=1)
    earlier = jnp.cumsum(per_row, axis=0) - per_row
    slot_index = jnp.sum(onehot * earlier[:, None, :], axis=2)
    in_slot = (
        slot_index[:, :, None] == jnp.arange(CAPACITY, dtype=jnp.int32)[None, None, :]
    ).astype(jnp.int32)
    chart = onehot[:, :, :, None] * in_slot[:, :, None, :]
    picker = jnp.sum(chart, axis=1).astype(jnp.bfloat16)
    outbound = jnp.einsum("rec,rd->ecd", picker, normed, preferred_element_type=jnp.float32).astype(
        jnp.bfloat16
    )
    expert_devs = lax.axis_size("expert")
    local_experts = experts // expert_devs
    model_width = normed.shape[1]
    outbound = outbound.reshape(expert_devs, local_experts, CAPACITY, model_width)
    inbound = lax.all_to_all(outbound, "expert", split_axis=0, concat_axis=0, tiled=True)
    gate_act = jnp.einsum("secd,edf->secf", inbound, w_gate, preferred_element_type=jnp.float32)
    upper = jnp.einsum("secd,edf->secf", inbound, w_up, preferred_element_type=jnp.float32)
    activated = (jax.nn.silu(gate_act) * upper).astype(jnp.bfloat16)
    down_terms = jnp.einsum("secf,efd->secd", activated, w_down, preferred_element_type=jnp.float32)
    summed = lax.psum(down_terms.astype(jnp.bfloat16), ("group", "seq")).astype(jnp.float32)
    col_width = summed.shape[3] // lax.axis_size("seq")
    my_cols = lax.dynamic_slice_in_dim(summed, lax.axis_index("seq") * col_width, col_width, 3)
    returned = lax.all_to_all(
        my_cols.astype(jnp.bfloat16), "expert", split_axis=0, concat_axis=0, tiled=True
    )
    returned = returned.reshape(experts, CAPACITY, returned.shape[3]).astype(jnp.float32)
    mixing = jnp.sum(gate_probs[:, :, None, None] * chart.astype(jnp.float32), axis=1)
    expert_mix = jnp.einsum("rec,ecd->rd", mixing, returned, precision=lax.Precision.HIGHEST)
    return (hidden + expert_mix).astype(jnp.bfloat16)


def solution(mesh):
    return jax.shard_map(
        shards,
        mesh=mesh,
        in_specs=(
            P("expert", "group", None),
            P("expert", "seq", "group", None),
            P("expert", "seq", "group", None),
            P("expert", "seq"),
            P("expert"),
            P("group", "seq"),
            P("expert", "seq"),
            P(),
            P(),
            P("expert", None),
            P("expert", None, ("group", "seq")),
            P("expert", None, ("group", "seq")),
            P("expert", ("group", "seq"), None),
        ),
        out_specs=P("expert", "seq"),
        check_vma=False,
    )
```

profile of v0, /device:TPU:0, one launch (start us, length us, event | category | flops | bytes accessed | tf_op | source)
XLA Modules:
  0.0 164.8 jit_solution(3506737250032493510)
XLA Ops:
  6.5 0.0 copy-start
  6.5 0.8 fusion.56
  7.3 0.7 fusion.55
  8.1 0.7 broadcast_multiply_fusion
  8.8 0.1 add.70
  8.8 0.1 add.71
  8.9 0.1 add.73
  9.0 0.7 add_compare_fusion
  9.8 0.0 copy-done
  9.8 1.0 fusion.64
  10.8 5.3 %all-gather.1 = f32[8,2,4]{2,1,0:T(2,128)S(1)} all-gather(f32[4,2,4]{2,1,0:T(2,128)S(1)} %get-tuple-element.22), channel_id=3, replica_groups=mesh['group'=4,'seq'=2,'expert'=4] {'seq'}, dimensions={0}, use_global_device_ids=true | all-gather | bytes 384 | tf_op jit(solution)/shard_map/all_gather | solution.py:14
  16.1 0.2 fusion.44
  16.3 1.2 fusion.29
  17.4 4.4 %all-gather = f32[8,2,4,128]{3,2,1,0:T(4,128)S(1)} all-gather(f32[4,2,4,128]{3,2,1,0:T(4,128)S(1)} %fusion.29), channel_id=2, replica_groups=mesh['group'=4,'seq'=2,'expert'=4] {'seq'}, dimensions={0}, use_global_device_ids=true | all-gather | bytes 49152 | tf_op jit(solution)/shard_map/all_gather | solution.py:14
  21.8 4.3 %all-gather.2 = f32[8,2,4]{2,1,0:T(2,128)S(1)} all-gather(f32[4,2,4]{2,1,0:T(2,128)S(1)} %fusion.44), channel_id=4, replica_groups=mesh['group'=4,'seq'=2,'expert'=4] {'seq'}, dimensions={0}, use_global_device_ids=true | all-gather | bytes 384 | tf_op jit(solution)/shard_map/all_gather | solution.py:14
  26.2 0.1 fusion.43
  26.3 2.8 %fusion.65 = f32[4,2048]{1,0:T(4,128)S(1)} fusion(bf16[4,1024]{1,0:T(4,128)(2,1)S(1)} %reshape.183, bf16[1024,2048]{1,0:T(8,128)(2,1)} %param.18), kind=kOutput, calls=%fused_computation.72 | convolution fusion | flops 16777216 | bytes 4235264 | tf_op jit(solution)/shard_map/dot_general | solution.py:78
  29.2 10.3 %psum.14 = f32[4,2048]{1,0:T(4,128)S(1)} all-reduce(f32[4,2048]{1,0:T(4,128)S(1)} %fusion.65), channel_id=1, replica_groups=mesh['group'=4,'seq'=2,'expert'=4] {'group'}, use_global_device_ids=true, to_apply=%region_2.3 | all-reduce | flops 8192 | bytes 65536 | tf_op jit(solution)/shard_map/psum | solution.py:79
  39.5 0.9 select_reduce_fusion
  40.4 0.7 convert_add_fusion
  41.1 4.6 %all_gather.27 = f32[4,4096]{1,0:T(4,128)S(1)} all-gather(f32[4,2048]{1,0:T(4,128)S(1)} %convert_add_fusion), channel_id=1, replica_groups=mesh['group'=4,'seq'=2,'expert'=4] {'seq'}, dimensions={1}, use_global_device_ids=true | all-gather | bytes 98304 | tf_op jit(solution)/shard_map/all_gather | solution.py:81
  45.7 0.7 convert_element_type.66
  46.4 0.1 multiply_reduce_fusion
  46.6 0.1 multiply_convert_fusion
  46.7 0.1 multiply_reduce_fusion.1
  46.7 0.2 convolution_convert_fusion
  47.0 0.8 copy.42
  47.7 5.4 %all-to-all-start = ((bf16[4,2,2,4096]{3,2,1,0:T(2,128)(2,1)}), bf16[4,2,2,4096]{3,2,1,0:T(2,128)(2,1)S(1)}, u32[]{:S(2)}, u32[]{:S(2)}) async-start(bf16[4,2,2,4096]{3,2,1,0:T(2,128)(2,1)} %bitcast.2), calls=%async_computation | async-start | bytes 262144 | tf_op jit(solution)/shard_map/all_to_all | solution.py:108
  53.1 0.0 all-reduce.2.cloned.1.call-start
  53.1 1.0 fusion.66
  54.1 0.9 multiply_reduce_fusion.2
  55.0 4.0 %all-to-all-done = bf16[4,2,2,4096]{3,2,1,0:T(2,128)(2,1)S(1)} async-done(((bf16[4,2,2,4096]{3,2,1,0:T(2,128)(2,1)}), bf16[4,2,2,4096]{3,2,1,0:T(2,128)(2,1)S(1)}, u32[]{:S(2)}, u32[]{:S(2)}) %all-to-all-start) | async-done | bytes 131104 | tf_op jit(solution)/shard_map/all_to_all | solution.py:108
  59.1 11.6 %fusion.12 = f32[4,2,2,1792]{3,0,2,1:T(4,128)S(1)} fusion(bf16[2,4096,1792]{2,1,0:T(8,128)(2,1)} %param.23, bf16[4,2,2,4096]{3,2,1,0:T(2,128)(2,1)S(1)} %all-to-all-done), kind=kOutput, calls=%fused_computation.9 | convolution fusion | flops 234881024 | bytes 29605888 | tf_op jit(solution)/shard_map/secd,edf->secf/dot_general | solution.py:109
  70.6 21.8 %fusion.9 = bf16[4,2,2,4096]{3,0,2,1:T(4,128)(2,1)} fusion(bf16[2,1792,4096]{2,1,0:T(8,128)(2,1)} %param.25, bf16[2,4096,1792]{2,1,0:T(8,128)(2,1)} %param.24, f32[4,2,2,1792]{3,0,2,1:T(4,128)S(1)} %fusion.12, bf16[4,2,2,4096]{3,2,1,0:T(2,128)(2,1)S(1)} %all-to-all-done), kind=kOutput, calls=%fused_computation.8 | convolution fusion | flops 469999616 | bytes 59097088 | tf_op jit(solution)/shard_map/secf,efd->secd/dot_general | solution.py:112
  92.4 0.0 all-reduce.2.cloned.1.call-update
  92.5 52.7 %all-reduce.2.cloned.1.call-done = bf16[4,2,2,4096]{3,0,2,1:T(4,128)(2,1)} async-done(((bf16[4,2,2,4096]{3,0,2,1:T(4,128)(2,1)}), bf16[4,2,2,4096]{3,0,2,1:T(4,128)(2,1)}) %all-reduce.2.cloned.1.call-update) | async-done | bytes 131088 | tf_op jit(solution)/shard_map/psum | solution.py:113
  145.2 0.9 convert_convert_fusion
  146.1 0.7 copy.37
  146.8 4.6 %all-to-all-start.1 = ((bf16[4,2,2,2048]{3,2,1,0:T(2,128)(2,1)}), bf16[4,2,2,2048]{3,2,1,0:T(2,128)(2,1)S(1)}, u32[]{:S(2)}, u32[]{:S(2)}) async-start(bf16[4,2,2,2048]{3,2,1,0:T(2,128)(2,1)} %copy.37), calls=%async_computation.1 | async-start | bytes 131072 | tf_op jit(solution)/shard_map/all_to_all | solution.py:116
  151.4 0.1 fusion.48
  151.5 5.7 %all-to-all-done.1 = bf16[4,2,2,2048]{3,2,1,0:T(2,128)(2,1)S(1)} async-done(((bf16[4,2,2,2048]{3,2,1,0:T(2,128)(2,1)}), bf16[4,2,2,2048]{3,2,1,0:T(2,128)(2,1)S(1)}, u32[]{:S(2)}, u32[]{:S(2)}) %all-to-all-start.1) | async-done | bytes 65568 | tf_op jit(solution)/shard_map/all_to_all | solution.py:116
  157.1 0.8 fusion.27
  (10 shorter events, 0.1 us)
Async XLA Ops:
  6.5 3.2 %copy-start = (bf16[4,128,2,128]{3,2,1,0:T(2,128)(2,1)S(1)}, bf16[4,128,2,128]{3,2,1,0:T(2,128)(2,1)}, u32[]{:S(2)}) copy-start(bf16[4,128,2,128]{3,2,1,0:T(2,128)(2,1)} %param.14) | copy-start | bytes 786436
  47.7 11.3 %all-to-all-start = ((bf16[4,2,2,4096]{3,2,1,0:T(2,128)(2,1)}), bf16[4,2,2,4096]{3,2,1,0:T(2,128)(2,1)S(1)}, u32[]{:S(2)}, u32[]{:S(2)}) async-start(bf16[4,2,2,4096]{3,2,1,0:T(2,128)(2,1)} %bitcast.2), calls=%async_computation | async-start | bytes 262144 | tf_op jit(solution)/shard_map/all_to_all | solution.py:108
  53.1 92.1 %all-reduce.2.cloned.1.call-start = ((), (), s32[]{:S(2)}) async-start(), calls=%async_computation.2 | async-start | bytes 262144 | tf_op jit(solution)/shard_map/psum | solution.py:113
  146.8 10.3 %all-to-all-start.1 = ((bf16[4,2,2,2048]{3,2,1,0:T(2,128)(2,1)}), bf16[4,2,2,2048]{3,2,1,0:T(2,128)(2,1)S(1)}, u32[]{:S(2)}, u32[]{:S(2)}) async-start(bf16[4,2,2,2048]{3,2,1,0:T(2,128)(2,1)} %copy.37), calls=%async_computation.1 | async-start | bytes 131072 | tf_op jit(solution)/shard_map/all_to_all | solution.py:116
Sparse Core Ops, SparseCore 0:
  92.6 52.6 all-reduce.1
where the time goes:
time: 166 us; the launch traced here: 165 us
  waiting for transfers between devices  62.5 us (38%)
  matrix products  40.5 us (24%)
  blocking collectives  28.9 us (17%)
  between operations  13.5 us (8%)
  starting transfers between devices  9.99 us (6%)
  other arithmetic  7.8 us (5%)
  local copies, waits for them, and re-layouts  1.72 us (1%)
    psum x1, waiting for transfers between devices, shards(): lax.psum(down_terms.astype(jnp.bfloat16), ('group', 'seq'))  52.7 us
    dot_general x1, matrix products, shards(): jnp.einsum('secf,efd->secd', activated, w_down, preferred_element_type=jn...  21.8 us
    all_gather x3, blocking collectives, combined_all(): everything = jax.tree.map(lambda part: lax.all_gather(part, axis), value)  14.1 us
    dot_general x1, matrix products, shards(): jnp.einsum('secd,edf->secf', inbound, w_gate, preferred_element_type=jnp....  11.6 us
    psum x1, blocking collectives, shards(): attention = lax.psum(partial_value, 'group')  10.3 us
    all_to_all x1, waiting for transfers between devices, shards(): lax.all_to_all(my_cols.astype(jnp.bfloat16), 'expert', split_axis=0, conc...  5.66 us
    all_to_all x1, starting transfers between devices, shards(): lax.all_to_all(outbound, 'expert', split_axis=0, concat_axis=0, tiled=True)  5.39 us
    all_to_all x1, starting transfers between devices, shards(): lax.all_to_all(my_cols.astype(jnp.bfloat16), 'expert', split_axis=0, conc...  4.59 us
  transfers between devices with their start and end apart: 3, of which 3 were waited for; matrix products, arithmetic and copies ran while one was open for 1% of the time, Pallas kernels for 0%

commit v1 on v0

v1 whole, which is shorter than its diff:
```python
import functools

import jax
import jax.numpy as jnp
from jax import lax
from jax.experimental import pallas as pl
from jax.experimental.pallas import tpu as pltpu
from jax.sharding import PartitionSpec as P

BLOCK = 16
LANES = 128
EPS = 1e-05
masked_score = -1e30
ROUTE = ("outer", "seq", "expert")
f32 = jnp.float32
bf16 = jnp.bfloat16
MIB = 1 << 20
LIMIT = 7 * MIB
WORK = 4_000_000_000

VMEM = pl.BlockSpec(memory_space=pltpu.VMEM)
SMEM = pl.BlockSpec(memory_space=pltpu.SMEM)
HBM = pl.BlockSpec(memory_space=pl.ANY)


def exchange(value, axes, keys):
    count = 1
    for axis in axes:
        count *= lax.axis_size(axis)
    return [lax.ppermute(value, axes, [(i, i ^ key) for i in range(count)]) for key in keys]


def call(body, out_shape, in_specs, limit, scratch=(), cost=WORK, **more):
    many = isinstance(out_shape, (tuple, list))
    return pl.pallas_call(
        body,
        out_shape=out_shape,
        in_specs=in_specs,
        out_specs=[VMEM] * len(out_shape) if many else VMEM,
        scratch_shapes=list(scratch),
        compiler_params=pltpu.CompilerParams(vmem_limit_bytes=limit),
        cost_estimate=pl.CostEstimate(flops=cost, bytes_accessed=0, transcendentals=0),
        **more,
    )


def attend_local(*refs, kv_local, held):
    inputs, sources, refs = refs[:5], refs[5 : 5 + held], refs[5 + held :]
    out_ref, targets, refs = refs[0], refs[1 : 1 + held], refs[1 + held :]
    slot_ref, len_ref, q_ref, k_ref, v_ref, sems = refs
    pairs = [*zip(inputs, refs), *zip(sources, targets)]
    copies = [pltpu.make_async_copy(a, b, sems.at[i]) for i, (a, b) in enumerate(pairs)]
    for copy in copies:
        copy.start()
    rows, heads, dim = q_ref.shape
    entries = k_ref.shape[1]
    per_kv = heads // kv_local
    width = LANES // (2 * rows)
    lane = lax.broadcasted_iota(jnp.int32, (1, entries), 1)
    inside = lane // kv_local
    block_at = inside // BLOCK
    head = lax.broadcasted_iota(jnp.int32, (heads, entries), 0)
    own_kv = (head // per_kv) == (lane % kv_local)
    tag = lax.broadcasted_iota(jnp.int32, (heads, LANES), 1) // width
    stats = jnp.zeros((heads, LANES), f32)
    for copy in copies[:2]:
        copy.wait()
    seen = []
    for r in range(rows):
        start = jnp.zeros((1, entries), jnp.int32)
        for s in range(slot_ref.shape[1]):
            start = jnp.where(block_at == s, slot_ref[r, s] * BLOCK, start)
        seen.append(own_kv & ((start + inside % BLOCK) < len_ref[r]))
    for copy in copies[2:5]:
        copy.wait()
    for r in range(rows):
        scores = lax.dot_general(
            q_ref[r], k_ref[r], (((1,), (1,)), ((), ())), preferred_element_type=f32
        ) * (dim**-0.5)
        masked = jnp.where(seen[r], scores, masked_score)
        highest = jnp.max(masked, axis=1, keepdims=True)
        probs = jnp.where(seen[r], jnp.exp(masked - highest), 0.0)
        total = jnp.sum(probs, axis=1, keepdims=True)
        out_ref[pl.ds(r * heads, heads), :] = jnp.dot(
            probs.astype(bf16), v_ref[r], preferred_element_type=f32
        )
        stats = jnp.where(tag == 2 * r, highest, stats)
        stats = jnp.where(tag == 2 * r + 1, total, stats)
    out_ref[pl.ds(rows * heads, heads), :] = stats
    for copy in copies[5:]:
        copy.wait()


def project(*refs, rows, heads, parts):
    packs, (w_ref, res_ref, out_ref) = refs[:parts], refs[parts:]
    width = LANES // (2 * rows)
    dim = packs[0].shape[1]
    stats = [p[pl.ds(rows * heads, heads), :] for p in packs]
    lane_head = lax.broadcasted_iota(jnp.int32, (heads, heads * dim), 1) // dim
    row_head = lax.broadcasted_iota(jnp.int32, (heads, heads * dim), 0)
    flat = []
    for r in range(rows):
        highs = [s[:, 2 * r * width : 2 * r * width + 1] for s in stats]
        totals = [s[:, (2 * r + 1) * width : (2 * r + 1) * width + 1] for s in stats]
        top = functools.reduce(jnp.maximum, highs)
        scales = [jnp.exp(h - top) for h in highs]
        total = sum(t * c for t, c in zip(totals, scales))
        mixed = sum(p[pl.ds(r * heads, heads), :] * c for p, c in zip(packs, scales))
        spread = jnp.concatenate([mixed / total] * heads, axis=1)
        kept = jnp.where(lane_head == row_head, spread, 0.0)
        flat.append(jnp.sum(kept, axis=0, keepdims=True))
    attended = jnp.concatenate(flat, axis=0).astype(bf16)
    partial = jnp.dot(attended, w_ref[...], preferred_element_type=f32)
    first = (lax.axis_index("outer") + lax.axis_index("inner") == 0).astype(f32)
    out_ref[...] = (partial + res_ref[...].astype(f32) * first).astype(bf16)


def halves(width, start=0):
    core = lax.axis_index("inner")
    mine = pl.multiple_of(start + core * width, LANES)
    other = pl.multiple_of(start + (1 - core) * width, LANES)
    return pl.ds(mine, width), pl.ds(other, width)


def add_two(a_ref, b_ref, out_ref):
    out_ref[...] = (a_ref[...].astype(f32) + b_ref[...].astype(f32)).astype(out_ref.dtype)


def normalize(*refs, spans, pairs):
    parts = refs[: spans * pairs]
    gain_ref, router_ref, routes_ref, pack_ref, hid_ref, full_ref = refs[spans * pairs :]
    rows, cols = parts[0].shape
    model = spans * cols
    me = lax.axis_index("seq")
    for k in range(spans):
        held = sum(parts[k + spans * j][...].astype(f32) for j in range(pairs))
        if k == 0:
            hid_ref[...] = held
        full_ref[:, pl.ds(pl.multiple_of((me ^ k) * cols, cols), cols)] = held
    full = full_ref[...]
    meansq = jnp.sum(full * full, axis=1, keepdims=True) * (1.0 / model)
    scaled = full * lax.rsqrt(meansq + EPS)
    gain = gain_ref[...].astype(f32)
    normed = jnp.concatenate(
        [
            scaled[:, j * LANES : (j + 1) * LANES] * gain[j : j + 1, :]
            for j in range(model // LANES)
        ],
        axis=1,
    ).astype(bf16)
    logits = lax.dot_general(
        normed, router_ref[...], (((1,), (1,)), ((), ())), preferred_element_type=f32
    )
    expert = lax.broadcasted_iota(jnp.int32, logits.shape, 1)
    topk = routes_ref.shape[0]
    row = lax.broadcasted_iota(jnp.int32, logits.shape, 0)
    named = []
    for k in range(topk):
        route = jnp.zeros(logits.shape, jnp.int32)
        for r in range(rows):
            route = jnp.where(row == r, routes_ref[k, r], route)
        named.append(expert == route)
    chosen = [jnp.sum(jnp.where(n, logits, 0.0), axis=1, keepdims=True) for n in named]
    top = functools.reduce(jnp.maximum, chosen)
    raised = [jnp.exp(c - top) for c in chosen]
    total = sum(raised)
    mixing = sum(jnp.where(n, e / total, 0.0) for n, e in zip(named, raised))
    coarse = mixing.astype(bf16)
    fine = (mixing - coarse.astype(f32)).astype(bf16)
    pack_ref[:, pl.ds(0, model)] = normed
    pack_ref[:, pl.ds(model, 2 * LANES)] = jnp.zeros((rows, 2 * LANES), bf16)
    pack_ref[:, pl.ds(model, logits.shape[1])] = coarse
    pack_ref[:, pl.ds(model + LANES, logits.shape[1])] = fine


def experts(*refs, slots, experts_all, spans, step, depth, cuts):
    packs = refs[:slots]
    (gate_ref, up_ref, down_ref, keep_ref, send_ref, x_ref, mix_ref, y_ref, ring_ref, sems) = refs[
        slots:
    ]
    rows = packs[0].shape[0]
    local, model, units = up_ref.shape
    steps = units // step
    part = model // cuts
    pieces = local * steps * cuts
    me = lax.axis_index("expert")

    def place(t):
        return t // steps, pl.ds((t % steps) * step, step)

    def fetch(p):
        e, at = place(p // cuts)
        slot = p % depth
        start = (p % cuts) * part
        return pltpu.make_async_copy(
            down_ref.at[e, at, pl.ds(start, part)], ring_ref.at[slot], sems.at[slot]
        )

    for p in range(min(depth, pieces)):
        fetch(p).start()
    lane = lax.broadcasted_iota(jnp.int32, (rows, experts_all), 1)
    for k in range(slots):
        y_ref[pl.ds(k * rows, rows), :] = packs[k][:, pl.ds(0, model)].astype(f32)
        mixing = packs[k][:, pl.ds(model, experts_all)].astype(f32) + packs[k][
            :, pl.ds(model + LANES, experts_all)
        ].astype(f32)
        for e in range(local):
            mine = jnp.where(lane == me * local + e, mixing, 0.0)
            mix_ref[e, pl.ds(k * rows, rows), :] = jnp.broadcast_to(
                jnp.sum(mine, axis=1, keepdims=True), (rows, LANES)
            )
    x_ref[...] = y_ref[...].astype(bf16)
    y_ref[...] = jnp.zeros_like(y_ref)

    def raise_up(t):
        e, at = place(t)
        gate = jnp.dot(x_ref[...], gate_ref[e, :, at], preferred_element_type=f32)
        upper = jnp.dot(x_ref[...], up_ref[e, :, at], preferred_element_type=f32)
        weight = mix_ref[e][:, 0:1]
        return (gate * jax.nn.sigmoid(gate) * upper * weight).astype(bf16)

    def bring_down(t, active):
        for p in range(t * cuts, (t + 1) * cuts):
            at = pl.ds((p % cuts) * part, part)
            fetch(p).wait()
            y_ref[:, at] += jnp.dot(active, ring_ref[p % depth], preferred_element_type=f32)
            if p + depth < pieces:
                fetch(p + depth).start()

    last = local * steps
    active = raise_up(0)
    for t in range(1, last):
        fresh = raise_up(t)
        bring_down(t - 1, active)
        active = fresh
    bring_down(last - 1, active)
    half = model // spans // 2
    for i in range(spans):
        mine, other = halves(half, 2 * half * i)
        keep_ref[i] = y_ref[:, mine]
        send_ref[i] = y_ref[:, other].astype(bf16)


def scatter(keep_ref, got_ref, out_ref, *, outers, slots):
    spans = keep_ref.shape[0]
    rows = out_ref.shape[1]
    me = lax.axis_index("expert")
    for i in range(spans):
        held = keep_ref[i] + got_ref[i].astype(f32)
        for k in range(slots):
            piece = held[k * rows : (k + 1) * rows].astype(bf16)
            for j in range(outers):
                out_ref[(j * spans + i) * slots + (me ^ k)] = piece


def sum_first(in_ref, out_ref):
    out_ref[...] = jnp.sum(in_ref[...].astype(f32), axis=0).astype(out_ref.dtype)


def finish(hid_ref, mine_ref, other_ref, out_ref):
    for mix_ref, cols in zip((mine_ref, other_ref), halves(mine_ref.shape[1])):
        out_ref[:, cols] = (hid_ref[:, cols] + mix_ref[...].astype(f32)).astype(bf16)


def shards(
    queries,
    keys,
    values,
    block_of_slot,
    lengths,
    out_proj,
    residual,
    norm_gain,
    router,
    routes,
    w_gate,
    w_up,
    w_down,
):
    rows, heads, dim = queries.shape
    span_len, kv_local = keys.shape[1:3]
    outers, spans, slots = (lax.axis_size(a) for a in ROUTE)
    cols = out_proj.shape[1]
    model = spans * cols
    shape = jax.ShapeDtypeStruct
    kept = [out_proj, residual, norm_gain.reshape(model // LANES, LANES), router.T]
    hbm = functools.partial(pltpu.with_memory_space_constraint, memory_space=pltpu.HBM)
    flat = (rows, span_len * kv_local, dim)
    pack, out_proj, residual, gain, router_t = call(
        functools.partial(attend_local, kv_local=kv_local, held=len(kept)),
        [shape((rows * heads + heads, dim), f32)]
        + [pltpu.VMEM(a.shape, a.dtype) for a in kept],
        [HBM] * (5 + len(kept)),
        2 * MIB,
        [
            pltpu.SMEM(block_of_slot.shape, jnp.int32),
            pltpu.SMEM(lengths.shape, jnp.int32),
            pltpu.VMEM(queries.shape, bf16),
            pltpu.VMEM(flat, bf16),
            pltpu.VMEM(flat, bf16),
            pltpu.SemaphoreType.DMA((5 + len(kept),)),
        ],
        name="attend",
    )(
        hbm(block_of_slot),
        hbm(lengths),
        hbm(queries),
        hbm(keys.reshape(flat)),
        hbm(values.reshape(flat)),
        *[hbm(a) for a in kept],
    )
    packs = [pack] + exchange(pack, ("seq",), range(1, spans))
    partial = call(
        functools.partial(project, rows=rows, heads=heads, parts=spans),
        shape((rows, cols), bf16),
        [VMEM] * (spans + 2),
        1 * MIB,
        name="project",
    )(*packs, out_proj, residual)
    (other,) = exchange(partial, ("inner",), [1])
    paired = call(
        add_two, shape((rows, cols), bf16), [VMEM] * 2, 1 * MIB, name="pair"
    )(partial, other)
    keys_xy = [j * 2 * spans + k for j in range(outers) for k in range(spans)]
    pieces = [paired] + exchange(paired, ("outer", "inner", "seq"), keys_xy[1:])
    packet, hidden = call(
        functools.partial(normalize, spans=spans, pairs=outers),
        (shape((rows, model + 2 * LANES), bf16), shape((rows, cols), f32)),
        [VMEM] * (len(pieces) + 2) + [SMEM],
        1 * MIB,
        [pltpu.VMEM((rows, model), f32)],
        name="normalize",
    )(*pieces, gain, router_t, routes.T)
    packets = [packet] + exchange(packet, ("expert",), range(1, slots))
    local, _, units = w_up.shape
    step = 256 if units % 256 == 0 else units
    cuts, depth = 4, 9
    depth = min(depth, local * (units // step) * cuts)
    everyone = rows * slots
    keep, send = call(
        functools.partial(
            experts,
            slots=slots,
            experts_all=router.shape[1],
            spans=spans,
            step=step,
            depth=depth,
            cuts=cuts,
        ),
        (
            pltpu.VMEM((spans, everyone, cols // 2), f32),
            pltpu.VMEM((spans, everyone, cols // 2), bf16),
        ),
        [VMEM] * slots + [VMEM, VMEM, HBM],
        LIMIT,
        [
            pltpu.VMEM((everyone, model), bf16),
            pltpu.VMEM((local, everyone, LANES), f32),
            pltpu.VMEM((everyone, model), f32),
            pltpu.VMEM((depth, step, model // cuts), bf16),
            pltpu.SemaphoreType.DMA((depth,)),
        ],
        name="experts",
    )(
        *[pltpu.with_memory_space_constraint(p, pltpu.VMEM) for p in packets],
        pltpu.with_memory_space_constraint(w_gate, pltpu.VMEM),
        pltpu.with_memory_space_constraint(w_up, pltpu.VMEM),
        pltpu.with_memory_space_constraint(w_down, pltpu.HBM),
    )
    (back,) = exchange(send, ("inner",), [1])
    packet = call(
        functools.partial(scatter, outers=outers, slots=slots),
        shape((outers * spans * slots, rows, cols // 2), bf16),
        [VMEM] * 2,
        1 * MIB,
        name="scatter",
    )(keep, back)
    arrived = lax.all_to_all(packet, ROUTE, 0, 0, tiled=True)
    mine = call(sum_first, shape((rows, cols // 2), bf16), [VMEM], 1 * MIB, name="total")(arrived)
    (other,) = exchange(mine, ("inner",), [1])
    return call(finish, shape((rows, cols), bf16), [VMEM] * 3, 1 * MIB, name="finish")(
        hidden, mine, other
    )


def solution(mesh):
    groups, spans, slots = (mesh.shape[a] for a in ("group", "seq", "expert"))
    group = ("outer", "inner")
    split = jax.sharding.Mesh(
        mesh.devices.reshape(groups // 2, 2, spans, slots), (*group, "seq", "expert")
    )
    return jax.shard_map(
        shards,
        mesh=split,
        in_specs=(
            P("expert", group, None),
            P("expert", "seq", group, None),
            P("expert", "seq", group, None),
            P("expert", "seq"),
            P("expert"),
            P(group, "seq"),
            P("expert", "seq"),
            P(),
            P(),
            P("expert", None),
            P("expert", None, (*group, "seq")),
            P("expert", None, (*group, "seq")),
            P("expert", (*group, "seq"), None),
        ),
        out_specs=P("expert", "seq"),
        check_vma=False,
    )
```

time: 166 us -> 56.4 us (0.34)
  waiting for transfers between devices: 62.5 us -> 13 us
  matrix products: 40.5 us -> 0 us
  Pallas kernels: 0 us -> 19.3 us
  blocking collectives: 28.9 us -> 12.3 us
  between operations: 13.5 us -> 0.13 us
  other arithmetic: 7.8 us -> 0.01 us
  local copies, waits for them, and re-layouts: 1.72 us -> 0.03 us
    psum x1 -> x0, waiting for transfers between devices: 52.7 us -> none  [shards(): lax.psum(down_terms.astype(jnp.bfloat16), ('group', 'seq'))]
    dot_general x8 -> x0, matrix products: 40.5 us -> none  [the longest x1 21.8 us: shards(): jnp.einsum('secf,efd->secd', activated, w_down, preferred_element_type=jn...]
    pallas_call x0 -> x8, Pallas kernels: none -> 19.3 us  [the longest x1 14.3 us: shards(): call(functools.partial(experts, slots=slots, experts_all=router.shape[1],...]
    all_gather x4 -> x0, blocking collectives: 18.7 us -> none  [the longest x3 14.1 us: combined_all(): everything = jax.tree.map(lambda part: lax.all_gather(part, axis), value)]
    ppermute x0 -> x10, waiting for transfers between devices: none -> 13 us  [exchange(): lax.ppermute(value, axes, [(i, i ^ key) for i in range(count)])]
    all_to_all x0 -> x1, blocking collectives: none -> 12.3 us  [shards(): arrived = lax.all_to_all(packet, ROUTE, 0, 0, tiled=True)]
    ppermute x0 -> x10, starting transfers between devices: none -> 11.4 us  [exchange(): lax.ppermute(value, axes, [(i, i ^ key) for i in range(count)])]
    psum x1 -> x0, blocking collectives: 10.3 us -> none  [shards(): attention = lax.psum(partial_value, 'group')]
  transfers between devices with their start and end apart: 3 -> 10, of which waited for: 3 -> 9; matrix products, arithmetic and copies ran while one was open for 1% -> 0% of each run, Pallas kernels for 0% -> 0%
where the time goes in v1:
time: 56.4 us; the launch traced here: 56.2 us
  Pallas kernels  19.3 us (34%)
  waiting for transfers between devices  13 us (23%)
  blocking collectives  12.3 us (22%)
  starting transfers between devices  11.4 us (20%)
    pallas_call x1, Pallas kernels, shards(): call(functools.partial(experts, slots=slots, experts_all=router.shape[1],...  14.3 us
    ppermute x10, waiting for transfers between devices, exchange(): lax.ppermute(value, axes, [(i, i ^ key) for i in range(count)])  13 us
    all_to_all x1, blocking collectives, shards(): arrived = lax.all_to_all(packet, ROUTE, 0, 0, tiled=True)  12.3 us
    ppermute x10, starting transfers between devices, exchange(): lax.ppermute(value, axes, [(i, i ^ key) for i in range(count)])  11.4 us
    pallas_call x1, Pallas kernels, shards(): call(functools.partial(attend_local, kv_local=kv_local, held=len(kept)),...  2.6 us
  transfers between devices with their start and end apart: 10, of which 9 were waited for; matrix products, arithmetic and copies ran while one was open for 0% of the time, Pallas kernels for 0%

profile of v1, /device:TPU:0, one launch (start us, length us, event | category | flops | bytes accessed | tf_op | source)
XLA Modules:
  0.0 56.2 jit_solution(10635493293366257636)
XLA Ops:
  0.0 0.0 copy-start.1
  0.0 0.0 slice-start
  0.0 0.0 slice-start.1
  0.0 0.0 copy-start
  0.0 2.6 %attend.1 = (f32[40,128]{1,0:T(8,128)S(1)}, bf16[1024,2048]{1,0:T(8,128)(2,1)S(1)}, bf16[4,2048]{1,0:T(4,128)(2,1)S(1)}, bf16[32,128]{1,0:T(8,128)(2,1)S(1)}, bf16[8,4096]{1,0:T(8,128)(2,1)S(1)}) custom-call(s32[4,8]{1,0:T(4,128)} %refs_0_.1, s32[4]{0:T(128)} %refs_1_.1, bf16[4,8,128]{2,1,0:T(8,128)(2,1)} %refs_2_.1, bf16[4,256,128]{2,1,0:T(8,128)(2,1)} %bitcast.8, ...), custom_call_target="tpu_custom_call" | custom-call | flops 4000000000 | tf_op jit(solution)/shard_map/attend/pallas_call | solution.py:289
  2.6 3.1 %collective-permute-start = (f32[40,128]{1,0:T(8,128)S(1)}, f32[40,128]{1,0:T(8,128)S(1)}, u32[]{:S(2)}, u32[]{:S(2)}) collective-permute-start(f32[40,128]{1,0:T(8,128)S(1)} %get-tuple-element.14.refs_0_), channel_id=1, source_target_pairs={{0,4},{4,0},{1,5},{5,1},{2,6},{6,2},{3,7},{7,3},{8,12},{12,8},{9,1... | collective-permute-start | bytes 61448 | tf_op jit(solution)/shard_map/ppermute | solution.py:30
  5.7 1.8 %collective-permute-done.refs_1_ = f32[40,128]{1,0:T(8,128)S(1)} collective-permute-done((f32[40,128]{1,0:T(8,128)S(1)}, f32[40,128]{1,0:T(8,128)S(1)}, u32[]{:S(2)}, u32[]{:S(2)}) %collective-permute-start) | collective-permute-done | bytes 20512 | tf_op jit(solution)/shard_map/ppermute | solution.py:30
  7.5 0.0 slice-start.2
  7.5 0.0 slice-start.3
  7.5 0.8 %project.1.a_ref = bf16[4,2048]{1,0:T(4,128)(2,1)S(1)} custom-call(f32[40,128]{1,0:T(8,128)S(1)} %get-tuple-element.14.refs_0_, f32[40,128]{1,0:T(8,128)S(1)} %collective-permute-done.refs_1_, bf16[1024,2048]{1,0:T(8,128)(2,1)S(1)} %get-tuple-element.15.refs_2_, bf16[4,2048]{1,0:T(4,128)(2,1)S(1)} %get-tuple-element.16.refs_3_), custom_call_target="tpu_custom_call" | custom-call | flops 4000000000 | tf_op jit(solution)/shard_map/project/pallas_call | solution.py:313
  8.3 0.0 slice-start.4
  8.3 0.0 slice-start.5
  8.3 0.1 collective-permute-start.1
  8.3 1.2 %collective-permute-done.1.b_ref = bf16[4,2048]{1,0:T(4,128)(2,1)S(1)} collective-permute-done((bf16[4,2048]{1,0:T(4,128)(2,1)S(1)}, bf16[4,2048]{1,0:T(4,128)(2,1)S(1)}, u32[]{:S(2)}, u32[]{:S(2)}) %collective-permute-start.1) | collective-permute-done | bytes 16416 | tf_op jit(solution)/shard_map/ppermute | solution.py:30
  9.5 3.0 %collective-permute-start.4 = (bf16[4,2048]{1,0:T(4,128)(2,1)S(1)}, bf16[4,2048]{1,0:T(4,128)(2,1)S(1)}, u32[]{:S(2)}, u32[]{:S(2)}) collective-permute-start(bf16[4,2048]{1,0:T(4,128)(2,1)S(1)} %pair.1.refs_0_), channel_id=1, source_target_pairs={{0,20},{4,16},{8,28},{12,24},{16,4},{20,0},{24,12},{28,8},{1,21},{... | collective-permute-start | bytes 49160 | tf_op jit(solution)/shard_map/ppermute | solution.py:30
  12.5 0.5 collective-permute-start.3
  13.1 0.1 collective-permute-start.2
  13.2 1.1 %collective-permute-done.4.refs_3_ = bf16[4,2048]{1,0:T(4,128)(2,1)S(1)} collective-permute-done((bf16[4,2048]{1,0:T(4,128)(2,1)S(1)}, bf16[4,2048]{1,0:T(4,128)(2,1)S(1)}, u32[]{:S(2)}, u32[]{:S(2)}) %collective-permute-start.4) | collective-permute-done | bytes 16416 | tf_op jit(solution)/shard_map/ppermute | solution.py:30
  14.3 2.0 %collective-permute-done.3.refs_2_ = bf16[4,2048]{1,0:T(4,128)(2,1)S(1)} collective-permute-done((bf16[4,2048]{1,0:T(4,128)(2,1)S(1)}, bf16[4,2048]{1,0:T(4,128)(2,1)S(1)}, u32[]{:S(2)}, u32[]{:S(2)}) %collective-permute-start.3) | collective-permute-done | bytes 16416 | tf_op jit(solution)/shard_map/ppermute | solution.py:30
  16.3 0.5 collective-permute-done.2.refs_1_
  16.8 0.0 copy-done.1
  16.8 0.0 slice-start.6
  16.8 0.9 %normalize.1 = (bf16[4,4352]{1,0:T(4,128)(2,1)S(1)}, f32[4,2048]{1,0:T(4,128)S(1)}) custom-call(bf16[4,2048]{1,0:T(4,128)(2,1)S(1)} %pair.1.refs_0_, bf16[4,2048]{1,0:T(4,128)(2,1)S(1)} %collective-permute-done.2.refs_1_, bf16[4,2048]{1,0:T(4,128)(2,1)S(1)} %collective-permute-done.3.refs_2_, bf16[4,2048]{1,0:T(4,128)(2,1)S(1)} %collective-permute-done.4.refs_3_, ...), custom_call_target="tpu_custom_call" | custom-call | flops 4000000000 | tf_op jit(solution)/shard_map/normalize/pallas_call | solution.py:326
  17.8 3.7 %collective-permute-start.7 = (bf16[4,4352]{1,0:T(4,128)(2,1)S(1)}, bf16[4,4352]{1,0:T(4,128)(2,1)S(1)}, u32[]{:S(2)}, u32[]{:S(2)}) collective-permute-start(bf16[4,4352]{1,0:T(4,128)(2,1)S(1)} %get-tuple-element.20.refs_0_), channel_id=1, source_target_pairs={{0,3},{1,2},{2,1},{3,0},{4,7},{5,6},{6,5},{7,4},{8,11},{9,10},{10,... | collective-permute-start | bytes 104456 | tf_op jit(solution)/shard_map/ppermute | solution.py:30
  21.4 0.0 collective-permute-start.6
  21.4 0.8 %collective-permute-start.5 = (bf16[4,4352]{1,0:T(4,128)(2,1)S(1)}, bf16[4,4352]{1,0:T(4,128)(2,1)S(1)}, u32[]{:S(2)}, u32[]{:S(2)}) collective-permute-start(bf16[4,4352]{1,0:T(4,128)(2,1)S(1)} %get-tuple-element.20.refs_0_), channel_id=1, source_target_pairs={{0,1},{1,0},{2,3},{3,2},{4,5},{5,4},{6,7},{7,6},{8,9},{9,8},{10,11... | collective-permute-start | bytes 104456 | tf_op jit(solution)/shard_map/ppermute | solution.py:30
  22.2 1.4 %collective-permute-done.7.refs_3_ = bf16[4,4352]{1,0:T(4,128)(2,1)S(1)} collective-permute-done((bf16[4,4352]{1,0:T(4,128)(2,1)S(1)}, bf16[4,4352]{1,0:T(4,128)(2,1)S(1)}, u32[]{:S(2)}, u32[]{:S(2)}) %collective-permute-start.7) | collective-permute-done | bytes 34848 | tf_op jit(solution)/shard_map/ppermute | solution.py:30
  23.7 2.6 %collective-permute-done.6.refs_2_ = bf16[4,4352]{1,0:T(4,128)(2,1)S(1)} collective-permute-done((bf16[4,4352]{1,0:T(4,128)(2,1)S(1)}, bf16[4,4352]{1,0:T(4,128)(2,1)S(1)}, u32[]{:S(2)}, u32[]{:S(2)}) %collective-permute-start.6) | collective-permute-done | bytes 34848 | tf_op jit(solution)/shard_map/ppermute | solution.py:30
  26.3 0.0 collective-permute-done.5.refs_1_
  26.3 0.0 slice-done
  26.3 0.0 slice-done.1
  26.3 0.0 copy-done
  26.3 0.0 slice-done.2
  26.3 0.0 slice-done.3
  26.3 0.0 slice-done.4
  26.3 0.0 slice-done.5
  26.3 0.0 slice-done.6
  26.4 14.3 %experts.1 = (f32[2,16,1024]{2,1,0:T(8,128)S(1)}, bf16[2,16,1024]{2,1,0:T(8,128)(2,1)S(1)}) custom-call(bf16[4,4352]{1,0:T(4,128)(2,1)S(1)} %get-tuple-element.20.refs_0_, bf16[4,4352]{1,0:T(4,128)(2,1)S(1)} %collective-permute-done.5.refs_1_, bf16[4,4352]{1,0:T(4,128)(2,1)S(1)} %collective-permute-done.6.refs_2_, ...), custom_call_target="tpu_custom_call" | custom-call | flops 4000000000 | tf_op jit(solution)/shard_map/experts/pallas_call | solution.py:340
  40.6 0.1 collective-permute-start.8
  40.7 1.2 %collective-permute-done.8.got_ref = bf16[2,16,1024]{2,1,0:T(8,128)(2,1)S(1)} collective-permute-done((bf16[2,16,1024]{2,1,0:T(8,128)(2,1)S(1)}, bf16[2,16,1024]{2,1,0:T(8,128)(2,1)S(1)}, u32[]{:S(2)}, u32[]{:S(2)}) %collective-permute-start.8) | collective-permute-done | bytes 65568 | tf_op jit(solution)/shard_map/ppermute | solution.py:30
  42.0 12.3 %all_to_all.5.in_ref = bf16[16,4,1024]{2,1,0:T(4,128)(2,1)S(1)} all-to-all(bf16[16,4,1024]{2,1,0:T(4,128)(2,1)S(1)} %scatter.1), channel_id=1, replica_groups=mesh['outer'=2,'inner'=2,'seq'=2,'expert'=4] {'outer','seq','expert'}, dimensions={0} | all-to-all | bytes 262144 | tf_op jit(solution)/shard_map/all_to_all | solution.py:378
  54.3 0.1 total.1.mine_ref
  54.4 0.1 collective-permute-start.9
  54.4 1.2 %collective-permute-done.9.other_ref = bf16[4,1024]{1,0:T(4,128)(2,1)S(1)} collective-permute-done((bf16[4,1024]{1,0:T(4,128)(2,1)S(1)}, bf16[4,1024]{1,0:T(4,128)(2,1)S(1)}, u32[]{:S(2)}, u32[]{:S(2)}) %collective-permute-start.9) | collective-permute-done | bytes 8224 | tf_op jit(solution)/shard_map/ppermute | solution.py:30
  55.6 0.6 %finish.1 = bf16[4,2048]{1,0:T(4,128)(2,1)} custom-call(f32[4,2048]{1,0:T(4,128)S(1)} %get-tuple-element.19.hid_ref, bf16[4,1024]{1,0:T(4,128)(2,1)S(1)} %total.1.mine_ref, bf16[4,1024]{1,0:T(4,128)(2,1)S(1)} %collective-permute-done.9.other_ref), custom_call_target="tpu_custom_call" | custom-call | flops 4000000000 | tf_op jit(solution)/shard_map/finish/pallas_call | solution.py:381
  (3 shorter events, 0.0 us)
Async XLA Ops:
  0.0 16.8 %copy-start.1 = (s32[4,2]{0,1:T(2,128)S(1)}, s32[4,2]{0,1:T(2,128)}, u32[]{:S(2)}) copy-start(s32[4,2]{0,1:T(2,128)} %param.22) | copy-start | bytes 100
  0.0 26.3 %slice-start = ((s8[29360128]{0:T(1024)(128)(4,1)}), s8[4194304]{0:T(1024)(128)(4,1)S(1)}, s32[]{:S(2)}) async-start(s8[29360128]{0:T(1024)(128)(4,1)} %bitcast.5), calls=%async_computation.1 | async-start | bytes 8388608
  0.0 26.3 %slice-start.1 = ((s8[29360128]{0:T(1024)(128)(4,1)}), s8[4194304]{0:T(1024)(128)(4,1)S(1)}, s32[]{:S(2)}) async-start(s8[29360128]{0:T(1024)(128)(4,1)} %bitcast.5), calls=%async_computation.2 | async-start | bytes 8388608
  0.0 26.3 %copy-start = (bf16[2,4096,1792]{2,1,0:T(8,128)(2,1)S(1)}, bf16[2,4096,1792]{2,1,0:T(8,128)(2,1)}, u32[]{:S(2)}) copy-start(bf16[2,4096,1792]{2,1,0:T(8,128)(2,1)} %refs_5_.3) | copy-start | bytes 88080384
  2.6 4.8 %collective-permute-start = (f32[40,128]{1,0:T(8,128)S(1)}, f32[40,128]{1,0:T(8,128)S(1)}, u32[]{:S(2)}, u32[]{:S(2)}) collective-permute-start(f32[40,128]{1,0:T(8,128)S(1)} %get-tuple-element.14.refs_0_), channel_id=1, source_target_pairs={{0,4},{4,0},{1,5},{5,1},{2,6},{6,2},{3,7},{7,3},{8,12},{12,8},{9,1... | collective-permute-start | bytes 61448 | tf_op jit(solution)/shard_map/ppermute | solution.py:30
  7.5 18.8 %slice-start.2 = ((s8[29360128]{0:T(1024)(128)(4,1)}), s8[4194304]{0:T(1024)(128)(4,1)S(1)}, s32[]{:S(2)}) async-start(s8[29360128]{0:T(1024)(128)(4,1)} %bitcast.5), calls=%async_computation.3 | async-start | bytes 8388608
  7.5 18.9 %slice-start.3 = ((s8[29360128]{0:T(1024)(128)(4,1)}), s8[4194304]{0:T(1024)(128)(4,1)S(1)}, s32[]{:S(2)}) async-start(s8[29360128]{0:T(1024)(128)(4,1)} %bitcast.5), calls=%async_computation.4 | async-start | bytes 8388608
  8.3 18.1 %slice-start.4 = ((s8[29360128]{0:T(1024)(128)(4,1)}), s8[4194304]{0:T(1024)(128)(4,1)S(1)}, s32[]{:S(2)}) async-start(s8[29360128]{0:T(1024)(128)(4,1)} %bitcast.5), calls=%async_computation.5 | async-start | bytes 8388608
  8.3 18.1 %slice-start.5 = ((s8[29360128]{0:T(1024)(128)(4,1)}), s8[4194304]{0:T(1024)(128)(4,1)S(1)}, s32[]{:S(2)}) async-start(s8[29360128]{0:T(1024)(128)(4,1)} %bitcast.5), calls=%async_computation.6 | async-start | bytes 8388608
  8.3 1.2 %collective-permute-start.1 = (bf16[4,2048]{1,0:T(4,128)(2,1)S(1)}, bf16[4,2048]{1,0:T(4,128)(2,1)S(1)}, u32[]{:S(2)}, u32[]{:S(2)}) collective-permute-start(bf16[4,2048]{1,0:T(4,128)(2,1)S(1)} %project.1.a_ref), channel_id=1, source_target_pairs={{0,8},{8,0},{1,9},{9,1},{2,10},{10,2},{3,11},{11,3},{4,12},{12,4},... | collective-permute-start | bytes 49160 | tf_op jit(solution)/shard_map/ppermute | solution.py:30
  9.5 4.7 %collective-permute-start.4 = (bf16[4,2048]{1,0:T(4,128)(2,1)S(1)}, bf16[4,2048]{1,0:T(4,128)(2,1)S(1)}, u32[]{:S(2)}, u32[]{:S(2)}) collective-permute-start(bf16[4,2048]{1,0:T(4,128)(2,1)S(1)} %pair.1.refs_0_), channel_id=1, source_target_pairs={{0,20},{4,16},{8,28},{12,24},{16,4},{20,0},{24,12},{28,8},{1,21},{... | collective-permute-start | bytes 49160 | tf_op jit(solution)/shard_map/ppermute | solution.py:30
  12.5 3.7 %collective-permute-start.3 = (bf16[4,2048]{1,0:T(4,128)(2,1)S(1)}, bf16[4,2048]{1,0:T(4,128)(2,1)S(1)}, u32[]{:S(2)}, u32[]{:S(2)}) collective-permute-start(bf16[4,2048]{1,0:T(4,128)(2,1)S(1)} %pair.1.refs_0_), channel_id=1, source_target_pairs={{0,16},{4,20},{8,24},{12,28},{16,0},{20,4},{24,8},{28,12},{1,17},{... | collective-permute-start | bytes 49160 | tf_op jit(solution)/shard_map/ppermute | solution.py:30
  13.1 3.7 %collective-permute-start.2 = (bf16[4,2048]{1,0:T(4,128)(2,1)S(1)}, bf16[4,2048]{1,0:T(4,128)(2,1)S(1)}, u32[]{:S(2)}, u32[]{:S(2)}) collective-permute-start(bf16[4,2048]{1,0:T(4,128)(2,1)S(1)} %pair.1.refs_0_), channel_id=1, source_target_pairs={{0,4},{4,0},{8,12},{12,8},{16,20},{20,16},{24,28},{28,24},{1,5},{5... | collective-permute-start | bytes 49160 | tf_op jit(solution)/shard_map/ppermute | solution.py:30
  16.8 9.5 %slice-start.6 = ((s8[29360128]{0:T(1024)(128)(4,1)}), s8[4194304]{0:T(1024)(128)(4,1)S(1)}, s32[]{:S(2)}) async-start(s8[29360128]{0:T(1024)(128)(4,1)} %bitcast.5), calls=%async_computation.7 | async-start | bytes 8388608
  17.8 5.9 %collective-permute-start.7 = (bf16[4,4352]{1,0:T(4,128)(2,1)S(1)}, bf16[4,4352]{1,0:T(4,128)(2,1)S(1)}, u32[]{:S(2)}, u32[]{:S(2)}) collective-permute-start(bf16[4,4352]{1,0:T(4,128)(2,1)S(1)} %get-tuple-element.20.refs_0_), channel_id=1, source_target_pairs={{0,3},{1,2},{2,1},{3,0},{4,7},{5,6},{6,5},{7,4},{8,11},{9,10},{10,... | collective-permute-start | bytes 104456 | tf_op jit(solution)/shard_map/ppermute | solution.py:30
  21.4 4.8 %collective-permute-start.6 = (bf16[4,4352]{1,0:T(4,128)(2,1)S(1)}, bf16[4,4352]{1,0:T(4,128)(2,1)S(1)}, u32[]{:S(2)}, u32[]{:S(2)}) collective-permute-start(bf16[4,4352]{1,0:T(4,128)(2,1)S(1)} %get-tuple-element.20.refs_0_), channel_id=1, source_target_pairs={{0,2},{1,3},{2,0},{3,1},{4,6},{5,7},{6,4},{7,5},{8,10},{9,11},{10,... | collective-permute-start | bytes 104456 | tf_op jit(solution)/shard_map/ppermute | solution.py:30
  21.4 4.8 %collective-permute-start.5 = (bf16[4,4352]{1,0:T(4,128)(2,1)S(1)}, bf16[4,4352]{1,0:T(4,128)(2,1)S(1)}, u32[]{:S(2)}, u32[]{:S(2)}) collective-permute-start(bf16[4,4352]{1,0:T(4,128)(2,1)S(1)} %get-tuple-element.20.refs_0_), channel_id=1, source_target_pairs={{0,1},{1,0},{2,3},{3,2},{4,5},{5,4},{6,7},{7,6},{8,9},{9,8},{10,11... | collective-permute-start | bytes 104456 | tf_op jit(solution)/shard_map/ppermute | solution.py:30
  40.6 1.3 %collective-permute-start.8 = (bf16[2,16,1024]{2,1,0:T(8,128)(2,1)S(1)}, bf16[2,16,1024]{2,1,0:T(8,128)(2,1)S(1)}, u32[]{:S(2)}, u32[]{:S(2)}) collective-permute-start(bf16[2,16,1024]{2,1,0:T(8,128)(2,1)S(1)} %get-tuple-element.22), channel_id=1, source_target_pairs={{0,8},{8,0},{1,9},{9,1},{2,10},{10,2},{3,11},{11,3},{4,12},{12,4},... | collective-permute-start | bytes 196616 | tf_op jit(solution)/shard_map/ppermute | solution.py:30
  54.4 1.2 %collective-permute-start.9 = (bf16[4,1024]{1,0:T(4,128)(2,1)S(1)}, bf16[4,1024]{1,0:T(4,128)(2,1)S(1)}, u32[]{:S(2)}, u32[]{:S(2)}) collective-permute-start(bf16[4,1024]{1,0:T(4,128)(2,1)S(1)} %total.1.mine_ref), channel_id=1, source_target_pairs={{0,8},{8,0},{1,9},{9,1},{2,10},{10,2},{3,11},{11,3},{4,12},{12,4},... | collective-permute-start | bytes 24584 | tf_op jit(solution)/shard_map/ppermute | solution.py:30

commit v2 on v1

--- a/solution.py
+++ b/solution.py
@@ -28,6 +28,33 @@
     for axis in axes:
         count *= lax.axis_size(axis)
     return [lax.ppermute(value, axes, [(i, i ^ key) for i in range(count)]) for key in keys]
+
+
+def split_exchange(value, axis, core):
+    count = lax.axis_size(axis)
+    held = []
+    for low in range(2, count, 2):
+        pairs = [
+            (c * count + i, c * count + (i ^ (low + 1 - c))) for c in range(2) for i in range(count)
+        ]
+        fetched = lax.ppermute(value, (core, axis), pairs)
+        held.append((fetched, exchange(fetched, (core,), [1])[0]))
+    (near,) = exchange(value, (axis,), [1])
+    return [near] + [part for pair in held for part in pair]
+
+
+def split_plane(value, outers, spans):
+    axes = ("outer", "inner", "seq")
+    if (outers, spans) != (2, 2):
+        keys = [j * 2 * spans + k for j in range(outers) for k in range(spans)]
+        return exchange(value, axes, keys[1:])
+    count = 2 * outers * spans
+    far = 2 * spans + 1
+    pairs = [(i, i ^ (1 if i // spans % 2 else far)) for i in range(count)]
+    fetched = lax.ppermute(value, axes, pairs)
+    (beside,) = exchange(value, axes, [2 * spans])
+    (swapped,) = exchange(fetched, ("inner",), [1])
+    return [fetched, beside, swapped]
 
 
 def call(body, out_shape, in_specs, limit, scratch=(), cost=WORK, **more):
@@ -173,7 +200,7 @@
     pack_ref[:, pl.ds(model + LANES, logits.shape[1])] = fine
 
 
-def experts(*refs, slots, experts_all, spans, step, depth, cuts):
+def experts(*refs, slots, spans, step, depth, cuts):
     packs = refs[:slots]
     (gate_ref, up_ref, down_ref, keep_ref, send_ref, x_ref, mix_ref, y_ref, ring_ref, sems) = refs[
         slots:
@@ -198,12 +225,14 @@
 
     for p in range(min(depth, pieces)):
         fetch(p).start()
-    lane = lax.broadcasted_iota(jnp.int32, (rows, experts_all), 1)
+    lane = lax.broadcasted_iota(jnp.int32, (rows, LANES), 1)
+    south = lax.axis_index("inner") == 0
     for k in range(slots):
-        y_ref[pl.ds(k * rows, rows), :] = packs[k][:, pl.ds(0, model)].astype(f32)
-        mixing = packs[k][:, pl.ds(model, experts_all)].astype(f32) + packs[k][
-            :, pl.ds(model + LANES, experts_all)
-        ].astype(f32)
+        pack = packs[k][...].astype(f32)
+        if k >= 2:
+            pack = jnp.where(south, packs[k ^ 1][...].astype(f32), pack)
+        y_ref[pl.ds(k * rows, rows), :] = pack[:, :model]
+        mixing = pack[:, model : model + LANES] + pack[:, model + LANES :]
         for e in range(local):
             mine = jnp.where(lane == me * local + e, mixing, 0.0)
             mix_ref[e, pl.ds(k * rows, rows), :] = jnp.broadcast_to(
@@ -321,8 +350,7 @@
     paired = call(
         add_two, shape((rows, cols), bf16), [VMEM] * 2, 1 * MIB, name="pair"
     )(partial, other)
-    keys_xy = [j * 2 * spans + k for j in range(outers) for k in range(spans)]
-    pieces = [paired] + exchange(paired, ("outer", "inner", "seq"), keys_xy[1:])
+    pieces = [paired] + split_plane(paired, outers, spans)
     packet, hidden = call(
         functools.partial(normalize, spans=spans, pairs=outers),
         (shape((rows, model + 2 * LANES), bf16), shape((rows, cols), f32)),
@@ -331,17 +359,16 @@
         [pltpu.VMEM((rows, model), f32)],
         name="normalize",
     )(*pieces, gain, router_t, routes.T)
-    packets = [packet] + exchange(packet, ("expert",), range(1, slots))
+    packets = [packet] + split_exchange(packet, "expert", "inner")
     local, _, units = w_up.shape
     step = 256 if units % 256 == 0 else units
-    cuts, depth = 4, 9
+    cuts, depth = 2, 5
     depth = min(depth, local * (units // step) * cuts)
     everyone = rows * slots
     keep, send = call(
         functools.partial(
             experts,
             slots=slots,
-            experts_all=router.shape[1],
             spans=spans,
             step=step,
             depth=depth,

time: 56.4 us -> 56.3 us (level)
  blocking collectives: 12.3 us -> 13.9 us
  starting transfers between devices: 11.4 us -> 10.5 us
    ppermute x10 -> x8, starting transfers between devices: 11.4 us -> 3.83 us  [exchange(): lax.ppermute(value, axes, [(i, i ^ key) for i in range(count)])]
    ppermute x0 -> x2, starting transfers between devices: none -> 6.68 us  [the longest x1 3.67 us: split_exchange(): fetched = lax.ppermute(value, (core, axis), pairs)]
    ppermute x10 -> x8, waiting for transfers between devices: 13 us -> 9.15 us  [exchange(): lax.ppermute(value, axes, [(i, i ^ key) for i in range(count)])]
    ppermute x0 -> x2, waiting for transfers between devices: none -> 3.31 us  [the longest x1 2.13 us: split_exchange(): fetched = lax.ppermute(value, (core, axis), pairs)]
    all_to_all x1, blocking collectives: 12.3 us -> 13.9 us  [shards(): arrived = lax.all_to_all(packet, ROUTE, 0, 0, tiled=True)]
  transfers between devices with their start and end apart: 10 -> 10, of which waited for: 9 -> 8; matrix products, arithmetic and copies ran while one was open for 0% -> 0% of each run, Pallas kernels for 0% -> 0%
where the time goes in v2:
time: 56.3 us; the launch traced here: 56.1 us
  Pallas kernels  19.1 us (34%)
  blocking collectives  13.9 us (25%)
  waiting for transfers between devices  12.5 us (22%)
  starting transfers between devices  10.5 us (19%)
    pallas_call x1, Pallas kernels, shards(): call(functools.partial(experts, slots=slots, spans=spans, step=step, dept...  14.1 us
    all_to_all x1, blocking collectives, shards(): arrived = lax.all_to_all(packet, ROUTE, 0, 0, tiled=True)  13.9 us
    ppermute x8, waiting for transfers between devices, exchange(): lax.ppermute(value, axes, [(i, i ^ key) for i in range(count)])  9.15 us
    ppermute x8, starting transfers between devices, exchange(): lax.ppermute(value, axes, [(i, i ^ key) for i in range(count)])  3.83 us
    ppermute x1, starting transfers between devices, split_exchange(): fetched = lax.ppermute(value, (core, axis), pairs)  3.67 us
    ppermute x1, starting transfers between devices, split_plane(): fetched = lax.ppermute(value, axes, pairs)  3.01 us
    pallas_call x1, Pallas kernels, shards(): call(functools.partial(attend_local, kv_local=kv_local, held=len(kept)),...  2.6 us
    ppermute x1, waiting for transfers between devices, split_exchange(): fetched = lax.ppermute(value, (core, axis), pairs)  2.13 us
  transfers between devices with their start and end apart: 10, of which 8 were waited for; matrix products, arithmetic and copies ran while one was open for 0% of the time, Pallas kernels for 0%

profile of v2, /device:TPU:0, one launch (start us, length us, event | category | flops | bytes accessed | tf_op | source)
XLA Modules:
  0.0 56.1 jit_solution(4795539623802529264)
XLA Ops:
  0.0 0.0 copy-start.1
  0.0 0.0 slice-start
  0.0 0.0 slice-start.1
  0.0 0.0 copy-start
  0.0 2.6 %attend.1 = (f32[40,128]{1,0:T(8,128)S(1)}, bf16[1024,2048]{1,0:T(8,128)(2,1)S(1)}, bf16[4,2048]{1,0:T(4,128)(2,1)S(1)}, bf16[32,128]{1,0:T(8,128)(2,1)S(1)}, bf16[8,4096]{1,0:T(8,128)(2,1)S(1)}) custom-call(s32[4,8]{1,0:T(4,128)} %refs_0_.1, s32[4]{0:T(128)} %refs_1_.1, bf16[4,8,128]{2,1,0:T(8,128)(2,1)} %refs_2_.1, bf16[4,256,128]{2,1,0:T(8,128)(2,1)} %bitcast.8, ...), custom_call_target="tpu_custom_call" | custom-call | flops 4000000000 | tf_op jit(solution)/shard_map/attend/pallas_call | solution.py:318
  2.6 3.1 %collective-permute-start = (f32[40,128]{1,0:T(8,128)S(1)}, f32[40,128]{1,0:T(8,128)S(1)}, u32[]{:S(2)}, u32[]{:S(2)}) collective-permute-start(f32[40,128]{1,0:T(8,128)S(1)} %get-tuple-element.14.refs_0_), channel_id=1, source_target_pairs={{0,4},{4,0},{1,5},{5,1},{2,6},{6,2},{3,7},{7,3},{8,12},{12,8},{9,1... | collective-permute-start | bytes 61448 | tf_op jit(solution)/shard_map/ppermute | solution.py:30
  5.7 1.8 %collective-permute-done.refs_1_ = f32[40,128]{1,0:T(8,128)S(1)} collective-permute-done((f32[40,128]{1,0:T(8,128)S(1)}, f32[40,128]{1,0:T(8,128)S(1)}, u32[]{:S(2)}, u32[]{:S(2)}) %collective-permute-start) | collective-permute-done | bytes 20512 | tf_op jit(solution)/shard_map/ppermute | solution.py:30
  7.5 0.0 slice-start.2
  7.5 0.0 slice-start.3
  7.5 0.8 %project.1.a_ref = bf16[4,2048]{1,0:T(4,128)(2,1)S(1)} custom-call(f32[40,128]{1,0:T(8,128)S(1)} %get-tuple-element.14.refs_0_, f32[40,128]{1,0:T(8,128)S(1)} %collective-permute-done.refs_1_, bf16[1024,2048]{1,0:T(8,128)(2,1)S(1)} %get-tuple-element.15.refs_2_, bf16[4,2048]{1,0:T(4,128)(2,1)S(1)} %get-tuple-element.16.refs_3_), custom_call_target="tpu_custom_call" | custom-call | flops 4000000000 | tf_op jit(solution)/shard_map/project/pallas_call | solution.py:342
  8.3 0.0 slice-start.4
  8.3 0.0 slice-start.5
  8.3 0.1 collective-permute-start.1
  8.3 1.2 %collective-permute-done.1.b_ref = bf16[4,2048]{1,0:T(4,128)(2,1)S(1)} collective-permute-done((bf16[4,2048]{1,0:T(4,128)(2,1)S(1)}, bf16[4,2048]{1,0:T(4,128)(2,1)S(1)}, u32[]{:S(2)}, u32[]{:S(2)}) %collective-permute-start.1) | collective-permute-done | bytes 16416 | tf_op jit(solution)/shard_map/ppermute | solution.py:30
  9.5 3.0 %collective-permute-start.2 = (bf16[4,2048]{1,0:T(4,128)(2,1)S(1)}, bf16[4,2048]{1,0:T(4,128)(2,1)S(1)}, u32[]{:S(2)}, u32[]{:S(2)}) collective-permute-start(bf16[4,2048]{1,0:T(4,128)(2,1)S(1)} %pair.1.refs_0_), channel_id=1, source_target_pairs={{0,20},{4,16},{8,12},{12,8},{16,4},{20,0},{24,28},{28,24},{1,21},{... | collective-permute-start | bytes 49160 | tf_op jit(solution)/shard_map/ppermute | solution.py:54
  12.5 0.5 collective-permute-start.3
  13.1 1.2 %collective-permute-done.2.refs_1_ = bf16[4,2048]{1,0:T(4,128)(2,1)S(1)} collective-permute-done((bf16[4,2048]{1,0:T(4,128)(2,1)S(1)}, bf16[4,2048]{1,0:T(4,128)(2,1)S(1)}, u32[]{:S(2)}, u32[]{:S(2)}) %collective-permute-start.2) | collective-permute-done | bytes 16416 | tf_op jit(solution)/shard_map/ppermute | solution.py:54
  14.3 0.0 collective-permute-start.4
  14.3 2.0 %collective-permute-done.3.refs_2_ = bf16[4,2048]{1,0:T(4,128)(2,1)S(1)} collective-permute-done((bf16[4,2048]{1,0:T(4,128)(2,1)S(1)}, bf16[4,2048]{1,0:T(4,128)(2,1)S(1)}, u32[]{:S(2)}, u32[]{:S(2)}) %collective-permute-start.3) | collective-permute-done | bytes 16416 | tf_op jit(solution)/shard_map/ppermute | solution.py:30
  16.3 0.0 collective-permute-done.4.refs_3_
  16.3 0.0 copy-done.1
  16.3 0.0 slice-start.6
  16.3 0.9 %normalize.1 = (bf16[4,4352]{1,0:T(4,128)(2,1)S(1)}, f32[4,2048]{1,0:T(4,128)S(1)}) custom-call(bf16[4,2048]{1,0:T(4,128)(2,1)S(1)} %pair.1.refs_0_, bf16[4,2048]{1,0:T(4,128)(2,1)S(1)} %collective-permute-done.2.refs_1_, bf16[4,2048]{1,0:T(4,128)(2,1)S(1)} %collective-permute-done.3.refs_2_, bf16[4,2048]{1,0:T(4,128)(2,1)S(1)} %collective-permute-done.4.refs_3_, ...), custom_call_target="tpu_custom_call" | custom-call | flops 4000000000 | tf_op jit(solution)/shard_map/normalize/pallas_call | solution.py:354
  17.2 3.7 %collective-permute-start.6 = (bf16[4,4352]{1,0:T(4,128)(2,1)S(1)}, bf16[4,4352]{1,0:T(4,128)(2,1)S(1)}, u32[]{:S(2)}, u32[]{:S(2)}) collective-permute-start(bf16[4,4352]{1,0:T(4,128)(2,1)S(1)} %get-tuple-element.20.refs_0_), channel_id=1, source_target_pairs={{0,3},{1,2},{2,1},{3,0},{8,10},{9,11},{10,8},{11,9},{4,7},{5,6},{6... | collective-permute-start | bytes 104456 | tf_op jit(solution)/shard_map/ppermute | solution.py:40
  20.9 0.0 collective-permute-start.5
  20.9 2.1 %collective-permute-done.6.refs_2_ = bf16[4,4352]{1,0:T(4,128)(2,1)S(1)} collective-permute-done((bf16[4,4352]{1,0:T(4,128)(2,1)S(1)}, bf16[4,4352]{1,0:T(4,128)(2,1)S(1)}, u32[]{:S(2)}, u32[]{:S(2)}) %collective-permute-start.6) | collective-permute-done | bytes 34848 | tf_op jit(solution)/shard_map/ppermute | solution.py:40
  23.0 0.0 collective-permute-start.7
  23.0 1.8 %collective-permute-done.5.refs_1_ = bf16[4,4352]{1,0:T(4,128)(2,1)S(1)} collective-permute-done((bf16[4,4352]{1,0:T(4,128)(2,1)S(1)}, bf16[4,4352]{1,0:T(4,128)(2,1)S(1)}, u32[]{:S(2)}, u32[]{:S(2)}) %collective-permute-start.5) | collective-permute-done | bytes 34848 | tf_op jit(solution)/shard_map/ppermute | solution.py:30
  24.8 0.0 collective-permute-done.7.refs_3_
  24.8 0.0 slice-done
  24.9 0.0 slice-done.1
  24.9 0.0 copy-done
  24.9 0.0 slice-done.2
  24.9 0.0 slice-done.3
  24.9 0.0 slice-done.4
  24.9 0.0 slice-done.5
  24.9 0.0 slice-done.6
  24.9 14.1 %experts.1 = (f32[2,16,1024]{2,1,0:T(8,128)S(1)}, bf16[2,16,1024]{2,1,0:T(8,128)(2,1)S(1)}) custom-call(bf16[4,4352]{1,0:T(4,128)(2,1)S(1)} %get-tuple-element.20.refs_0_, bf16[4,4352]{1,0:T(4,128)(2,1)S(1)} %collective-permute-done.5.refs_1_, bf16[4,4352]{1,0:T(4,128)(2,1)S(1)} %collective-permute-done.6.refs_2_, ...), custom_call_target="tpu_custom_call" | custom-call | flops 4000000000 | tf_op jit(solution)/shard_map/experts/pallas_call | solution.py:368
  39.0 0.1 collective-permute-start.8
  39.1 1.2 %collective-permute-done.8.got_ref = bf16[2,16,1024]{2,1,0:T(8,128)(2,1)S(1)} collective-permute-done((bf16[2,16,1024]{2,1,0:T(8,128)(2,1)S(1)}, bf16[2,16,1024]{2,1,0:T(8,128)(2,1)S(1)}, u32[]{:S(2)}, u32[]{:S(2)}) %collective-permute-start.8) | collective-permute-done | bytes 65568 | tf_op jit(solution)/shard_map/ppermute | solution.py:30
  40.3 13.9 %all_to_all.5.in_ref = bf16[16,4,1024]{2,1,0:T(4,128)(2,1)S(1)} all-to-all(bf16[16,4,1024]{2,1,0:T(4,128)(2,1)S(1)} %scatter.1), channel_id=1, replica_groups=mesh['outer'=2,'inner'=2,'seq'=2,'expert'=4] {'outer','seq','expert'}, dimensions={0} | all-to-all | bytes 262144 | tf_op jit(solution)/shard_map/all_to_all | solution.py:405
  54.2 0.1 total.1.mine_ref
  54.3 0.1 collective-permute-start.9
  54.4 1.2 %collective-permute-done.9.other_ref = bf16[4,1024]{1,0:T(4,128)(2,1)S(1)} collective-permute-done((bf16[4,1024]{1,0:T(4,128)(2,1)S(1)}, bf16[4,1024]{1,0:T(4,128)(2,1)S(1)}, u32[]{:S(2)}, u32[]{:S(2)}) %collective-permute-start.9) | collective-permute-done | bytes 8224 | tf_op jit(solution)/shard_map/ppermute | solution.py:30
  55.5 0.6 %finish.1 = bf16[4,2048]{1,0:T(4,128)(2,1)} custom-call(f32[4,2048]{1,0:T(4,128)S(1)} %get-tuple-element.19.hid_ref, bf16[4,1024]{1,0:T(4,128)(2,1)S(1)} %total.1.mine_ref, bf16[4,1024]{1,0:T(4,128)(2,1)S(1)} %collective-permute-done.9.other_ref), custom_call_target="tpu_custom_call" | custom-call | flops 4000000000 | tf_op jit(solution)/shard_map/finish/pallas_call | solution.py:408
  (3 shorter events, 0.0 us)
Async XLA Ops:
  0.0 16.3 %copy-start.1 = (s32[4,2]{0,1:T(2,128)S(1)}, s32[4,2]{0,1:T(2,128)}, u32[]{:S(2)}) copy-start(s32[4,2]{0,1:T(2,128)} %param.22) | copy-start | bytes 100
  0.0 24.8 %slice-start = ((s8[29360128]{0:T(1024)(128)(4,1)}), s8[4194304]{0:T(1024)(128)(4,1)S(1)}, s32[]{:S(2)}) async-start(s8[29360128]{0:T(1024)(128)(4,1)} %bitcast.5), calls=%async_computation.1 | async-start | bytes 8388608
  0.0 24.8 %slice-start.1 = ((s8[29360128]{0:T(1024)(128)(4,1)}), s8[4194304]{0:T(1024)(128)(4,1)S(1)}, s32[]{:S(2)}) async-start(s8[29360128]{0:T(1024)(128)(4,1)} %bitcast.5), calls=%async_computation.2 | async-start | bytes 8388608
  0.0 24.9 %copy-start = (bf16[2,4096,1792]{2,1,0:T(8,128)(2,1)S(1)}, bf16[2,4096,1792]{2,1,0:T(8,128)(2,1)}, u32[]{:S(2)}) copy-start(bf16[2,4096,1792]{2,1,0:T(8,128)(2,1)} %refs_5_.3) | copy-start | bytes 88080384
  2.6 4.8 %collective-permute-start = (f32[40,128]{1,0:T(8,128)S(1)}, f32[40,128]{1,0:T(8,128)S(1)}, u32[]{:S(2)}, u32[]{:S(2)}) collective-permute-start(f32[40,128]{1,0:T(8,128)S(1)} %get-tuple-element.14.refs_0_), channel_id=1, source_target_pairs={{0,4},{4,0},{1,5},{5,1},{2,6},{6,2},{3,7},{7,3},{8,12},{12,8},{9,1... | collective-permute-start | bytes 61448 | tf_op jit(solution)/shard_map/ppermute | solution.py:30
  7.5 17.4 %slice-start.2 = ((s8[29360128]{0:T(1024)(128)(4,1)}), s8[4194304]{0:T(1024)(128)(4,1)S(1)}, s32[]{:S(2)}) async-start(s8[29360128]{0:T(1024)(128)(4,1)} %bitcast.5), calls=%async_computation.3 | async-start | bytes 8388608
  7.5 17.4 %slice-start.3 = ((s8[29360128]{0:T(1024)(128)(4,1)}), s8[4194304]{0:T(1024)(128)(4,1)S(1)}, s32[]{:S(2)}) async-start(s8[29360128]{0:T(1024)(128)(4,1)} %bitcast.5), calls=%async_computation.4 | async-start | bytes 8388608
  8.3 16.6 %slice-start.4 = ((s8[29360128]{0:T(1024)(128)(4,1)}), s8[4194304]{0:T(1024)(128)(4,1)S(1)}, s32[]{:S(2)}) async-start(s8[29360128]{0:T(1024)(128)(4,1)} %bitcast.5), calls=%async_computation.5 | async-start | bytes 8388608
  8.3 16.6 %slice-start.5 = ((s8[29360128]{0:T(1024)(128)(4,1)}), s8[4194304]{0:T(1024)(128)(4,1)S(1)}, s32[]{:S(2)}) async-start(s8[29360128]{0:T(1024)(128)(4,1)} %bitcast.5), calls=%async_computation.6 | async-start | bytes 8388608
  8.3 1.2 %collective-permute-start.1 = (bf16[4,2048]{1,0:T(4,128)(2,1)S(1)}, bf16[4,2048]{1,0:T(4,128)(2,1)S(1)}, u32[]{:S(2)}, u32[]{:S(2)}) collective-permute-start(bf16[4,2048]{1,0:T(4,128)(2,1)S(1)} %project.1.a_ref), channel_id=1, source_target_pairs={{0,8},{8,0},{1,9},{9,1},{2,10},{10,2},{3,11},{11,3},{4,12},{12,4},... | collective-permute-start | bytes 49160 | tf_op jit(solution)/shard_map/ppermute | solution.py:30
  9.5 4.7 %collective-permute-start.2 = (bf16[4,2048]{1,0:T(4,128)(2,1)S(1)}, bf16[4,2048]{1,0:T(4,128)(2,1)S(1)}, u32[]{:S(2)}, u32[]{:S(2)}) collective-permute-start(bf16[4,2048]{1,0:T(4,128)(2,1)S(1)} %pair.1.refs_0_), channel_id=1, source_target_pairs={{0,20},{4,16},{8,12},{12,8},{16,4},{20,0},{24,28},{28,24},{1,21},{... | collective-permute-start | bytes 49160 | tf_op jit(solution)/shard_map/ppermute | solution.py:54
  12.5 3.7 %collective-permute-start.3 = (bf16[4,2048]{1,0:T(4,128)(2,1)S(1)}, bf16[4,2048]{1,0:T(4,128)(2,1)S(1)}, u32[]{:S(2)}, u32[]{:S(2)}) collective-permute-start(bf16[4,2048]{1,0:T(4,128)(2,1)S(1)} %pair.1.refs_0_), channel_id=1, source_target_pairs={{0,16},{4,20},{8,24},{12,28},{16,0},{20,4},{24,8},{28,12},{1,17},{... | collective-permute-start | bytes 49160 | tf_op jit(solution)/shard_map/ppermute | solution.py:30
  14.3 2.0 %collective-permute-start.4 = (bf16[4,2048]{1,0:T(4,128)(2,1)S(1)}, bf16[4,2048]{1,0:T(4,128)(2,1)S(1)}, u32[]{:S(2)}, u32[]{:S(2)}) collective-permute-start(bf16[4,2048]{1,0:T(4,128)(2,1)S(1)} %collective-permute-done.2.refs_1_), channel_id=1, source_target_pairs={{0,8},{8,0},{1,9},{9,1},{2,10},{10,2},{3,11},{11,3},{4,12},{12,4},... | collective-permute-start | bytes 49160 | tf_op jit(solution)/shard_map/ppermute | solution.py:30
  16.3 8.6 %slice-start.6 = ((s8[29360128]{0:T(1024)(128)(4,1)}), s8[4194304]{0:T(1024)(128)(4,1)S(1)}, s32[]{:S(2)}) async-start(s8[29360128]{0:T(1024)(128)(4,1)} %bitcast.5), calls=%async_computation.7 | async-start | bytes 8388608
  17.2 5.8 %collective-permute-start.6 = (bf16[4,4352]{1,0:T(4,128)(2,1)S(1)}, bf16[4,4352]{1,0:T(4,128)(2,1)S(1)}, u32[]{:S(2)}, u32[]{:S(2)}) collective-permute-start(bf16[4,4352]{1,0:T(4,128)(2,1)S(1)} %get-tuple-element.20.refs_0_), channel_id=1, source_target_pairs={{0,3},{1,2},{2,1},{3,0},{8,10},{9,11},{10,8},{11,9},{4,7},{5,6},{6... | collective-permute-start | bytes 104456 | tf_op jit(solution)/shard_map/ppermute | solution.py:40
  20.9 3.9 %collective-permute-start.5 = (bf16[4,4352]{1,0:T(4,128)(2,1)S(1)}, bf16[4,4352]{1,0:T(4,128)(2,1)S(1)}, u32[]{:S(2)}, u32[]{:S(2)}) collective-permute-start(bf16[4,4352]{1,0:T(4,128)(2,1)S(1)} %get-tuple-element.20.refs_0_), channel_id=1, source_target_pairs={{0,1},{1,0},{2,3},{3,2},{4,5},{5,4},{6,7},{7,6},{8,9},{9,8},{10,11... | collective-permute-start | bytes 104456 | tf_op jit(solution)/shard_map/ppermute | solution.py:30
  23.0 1.8 %collective-permute-start.7 = (bf16[4,4352]{1,0:T(4,128)(2,1)S(1)}, bf16[4,4352]{1,0:T(4,128)(2,1)S(1)}, u32[]{:S(2)}, u32[]{:S(2)}) collective-permute-start(bf16[4,4352]{1,0:T(4,128)(2,1)S(1)} %collective-permute-done.6.refs_2_), channel_id=1, source_target_pairs={{0,8},{8,0},{1,9},{9,1},{2,10},{10,2},{3,11},{11,3},{4,12},{12,4},... | collective-permute-start | bytes 104456 | tf_op jit(solution)/shard_map/ppermute | solution.py:30
  39.0 1.3 %collective-permute-start.8 = (bf16[2,16,1024]{2,1,0:T(8,128)(2,1)S(1)}, bf16[2,16,1024]{2,1,0:T(8,128)(2,1)S(1)}, u32[]{:S(2)}, u32[]{:S(2)}) collective-permute-start(bf16[2,16,1024]{2,1,0:T(8,128)(2,1)S(1)} %get-tuple-element.22), channel_id=1, source_target_pairs={{0,8},{8,0},{1,9},{9,1},{2,10},{10,2},{3,11},{11,3},{4,12},{12,4},... | collective-permute-start | bytes 196616 | tf_op jit(solution)/shard_map/ppermute | solution.py:30
  54.3 1.2 %collective-permute-start.9 = (bf16[4,1024]{1,0:T(4,128)(2,1)S(1)}, bf16[4,1024]{1,0:T(4,128)(2,1)S(1)}, u32[]{:S(2)}, u32[]{:S(2)}) collective-permute-start(bf16[4,1024]{1,0:T(4,128)(2,1)S(1)} %total.1.mine_ref), channel_id=1, source_target_pairs={{0,8},{8,0},{1,9},{9,1},{2,10},{10,2},{3,11},{11,3},{4,12},{12,4},... | collective-permute-start | bytes 24584 | tf_op jit(solution)/shard_map/ppermute | solution.py:30
